TPU v7x, 32 devices: a whole 2x2x4 slice. The times are simulated.
32 devices in a mesh: plane: 4 (over y, x), tile: 8 (over z, core).
Axes of the slice: x: 2, y: 2, z: 4, core: 2. Of those that a mesh axis runs over, the one named last changes fastest.
Arguments:
- visibility: float32 [2, 65536], P(None, ('plane', 'tile')), may hold values from -6 to 6
- target: int32 [65536, 1], P(('plane', 'tile')), may hold values from 0 to 31; in each aligned block of 2048 rows (0 to 2047, 2048 to 4095, ...) at most 128 rows name the same one
- offset: int32 [65536], P(('plane', 'tile')), may hold values from 0 to 2097151
- taps: float32 [8], replicated, may hold values from 0.1 to 1
- w_plane: float32 [4], P('plane'), may hold values from -300 to 300
Outputs:
- dirty_image: float32 [4096, 4096], P('plane', 'tile')
Inputs may be any that keep to these rules, and one draw needn't show every extreme that they name: `target`: among the rows of one device no value occurs more than 128 times, and some value occurs exactly 128 times.
All inputs are finite; a program needn't handle non-finite values.
Results may differ from a plain program's by a relative error of at most 0.0042.
Values sent between devices are 32-bit elements; how exact they have to be, the bound alone decides.
A program may use at most 128 MiB of HBM per device.

v0:
```python
import functools
import math

import jax
import jax.numpy as jnp
import numpy as np
from jax import lax
from jax.experimental import pallas as pl
from jax.experimental.pallas import tpu as pltpu
from jax.sharding import PartitionSpec as P

G = 4096
LANES = 128
WINDOW = 256
DIGITS = G // WINDOW
BLOCK = 64
PIECE = 4
WIDE = 1024
HALF = 512
NARROW = 256
MESH = pl.DeviceIdType.MESH


def fitted(function, terms):
    nodes = np.cos((np.arange(400) + 0.5) * np.pi / 400)
    square = 0.125 * (nodes + 1.0)
    table = np.polynomial.chebyshev.Chebyshev.fit(
        square, function(np.sqrt(square)), terms - 1, domain=[0.0, 0.25]
    )
    return [float(v) for v in table.convert(kind=np.polynomial.Polynomial).coef]


COS_COEF = fitted(lambda x: np.cos(2.0 * np.pi * x), 7)
SIN_COEF = fitted(lambda x: np.sin(2.0 * np.pi * x) / x, 6)


SHORT_COS = fitted(lambda x: np.cos(2.0 * np.pi * x), 6)
SHORT_SIN = fitted(lambda x: np.sin(2.0 * np.pi * x) / x, 5)


def horner(coefficients, x):
    total = coefficients[-1]
    for value in coefficients[-2::-1]:
        total = total * x + value
    return total


def turn(cycles, cos_terms=COS_COEF, sin_terms=SIN_COEF):
    part = cycles - jnp.round(cycles)
    square = part * part
    return horner(cos_terms, square), part * horner(sin_terms, square)


def pieces(value):
    high = value.astype(jnp.bfloat16).astype(jnp.float32)
    rest = value - high
    middle = rest.astype(jnp.bfloat16).astype(jnp.float32)
    return high, middle, rest - middle


def strict_upper(n):
    return jnp.where(
        lax.broadcasted_iota(jnp.int32, (n, n), 0) < lax.broadcasted_iota(jnp.int32, (n, n), 1),
        1.0,
        0.0,
    ).astype(jnp.bfloat16)


NT = (((1,), (1,)), ((), ()))


def flip(value, bits):
    bit = 1
    while bit <= bits:
        if bits & bit:
            value = value + bit - 2 * bit * lax.rem(value // bit, 2)
        bit *= 2
    return value


def front_kernel(
    windows, tiles, jumps, vis_ref, target_ref, offset_ref, w_ref, out_ref, level_ref,
    lhs_ref, rhs_ref, left_ref, right_ref, send_ref, got_ref, ring_ref,
    send_sem, got_sem, pass_sem, ring_sem,
):
    devices = send_ref.shape[0]
    plane, tile = lax.axis_index("plane"), lax.axis_index("tile")
    mine = plane * tiles + tile
    barrier = pltpu.get_barrier_semaphore()

    def seat(device):
        return {"plane": device // tiles, "tile": lax.rem(device, tiles)}

    @pl.loop(1, devices)
    def _(i):
        pl.semaphore_signal(
            barrier, inc=1, device_id=seat(lax.rem(mine + i, devices)), device_id_type=MESH
        )

    blocks = target_ref.shape[0]
    upper = strict_upper(LANES)
    line = lax.broadcasted_iota(jnp.int32, (devices, LANES), 0)
    slot = lax.broadcasted_iota(jnp.int32, (LANES, LANES), 0).astype(jnp.float32)
    carry = jnp.zeros((devices, 1), jnp.float32)
    for k in range(blocks):
        part = slice(k * LANES, (k + 1) * LANES)
        hit = line == target_ref[k : k + 1, :]
        hot = jnp.where(hit, 1.0, 0.0)
        before = jnp.dot(hot.astype(jnp.bfloat16), upper, preferred_element_type=jnp.float32)
        rank = jnp.sum(hot * (before + carry), axis=0, keepdims=True)
        carry = carry + jnp.sum(hot, axis=1, keepdims=True)
        rhs_ref[:, part] = jnp.where(slot == rank, 1.0, 0.0).astype(jnp.bfloat16)
        rows = (
            vis_ref[0, k : k + 1, :],
            vis_ref[1, k : k + 1, :],
            offset_ref[k : k + 1, :].astype(jnp.float32) + 1.0,
        )
        for p, row in enumerate(rows):
            for n, value in enumerate(pieces(row)):
                at = (p * 3 + n) * devices
                lhs_ref[at : at + devices, part] = jnp.where(hit, value, 0.0).astype(jnp.bfloat16)
    total = lax.dot_general(lhs_ref[...], rhs_ref[...], NT, preferred_element_type=jnp.float32)
    for p in range(3):
        at = p * 3 * devices
        send_ref[:, p, :] = (
            total[at : at + devices]
            + total[at + devices : at + 2 * devices]
            + total[at + 2 * devices : at + 3 * devices]
        )
    send_ref[:, 3, :] = jnp.full((devices, LANES), w_ref[0], jnp.float32)
    got_ref[mine] = send_ref[mine]
    pl.semaphore_wait(barrier, devices - 1)

    def post(source, target):
        return pltpu.make_async_remote_copy(
            src_ref=send_ref.at[target],
            dst_ref=got_ref.at[source],
            send_sem=send_sem.at[target],
            recv_sem=got_sem.at[source],
            device_id=seat(target),
            device_id_type=MESH,
        )

    @pl.loop(1, devices)
    def _(i):
        post(mine, lax.rem(mine + i, devices)).start()

    @pl.loop(1, devices)
    def _(i):
        post(lax.rem(mine + devices - i, devices), mine).wait_recv()

    for k in range(level_ref.shape[0]):
        near, far = flip(plane, jumps[0][k]), flip(plane, jumps[1][k])
        core = lax.rem(tile, 2)
        origin = (near * (1 - core) + far * core) * tiles + tile
        level_ref[k : k + 1, :] = got_ref[origin, 3:4, :]

    rows = out_ref.shape[2]
    encoded = got_ref[:, 2, :]
    row = jnp.floor((encoded - 1.0) * (1.0 / G))
    lower = jnp.where(
        lax.broadcasted_iota(jnp.int32, (devices, devices), 0)
        > lax.broadcasted_iota(jnp.int32, (devices, devices), 1),
        1.0,
        0.0,
    ).astype(jnp.bfloat16)
    position = jnp.full(row.shape, -1.0, jnp.float32)
    for w in range(windows):
        member = jnp.where((row >= w * WINDOW) & (row < (w + 1) * WINDOW), 1.0, 0.0)
        flags = member.astype(jnp.bfloat16)
        inside = jnp.dot(flags, upper, preferred_element_type=jnp.float32)
        ahead = jnp.sum(
            jnp.dot(lower, flags, preferred_element_type=jnp.float32), axis=1, keepdims=True
        )
        place = inside + ahead
        if w == 1:
            place = rows * LANES - 1 - place
        position = jnp.where(member > 0.0, place, position)
    high = jnp.floor(position * (1.0 / LANES))
    low = position - high * LANES
    line = lax.broadcasted_iota(jnp.int32, (rows, LANES), 0).astype(jnp.float32)
    parts = [pieces(got_ref[:, 0, :]), pieces(got_ref[:, 1, :]), pieces(encoded)]
    for k in range(devices):
        part = slice(k * LANES, (k + 1) * LANES)
        hit = line == high[k : k + 1, :]
        right_ref[:, part] = jnp.where(slot == low[k : k + 1, :], 1.0, 0.0).astype(jnp.bfloat16)
        for p in range(3):
            for n in range(3):
                at = (p * 3 + n) * rows
                left_ref[at : at + rows, part] = jnp.where(
                    hit, parts[p][n][k : k + 1, :], 0.0
                ).astype(jnp.bfloat16)
    total = lax.dot_general(left_ref[...], right_ref[...], NT, preferred_element_type=jnp.float32)
    for p in range(3):
        at = p * 3 * rows
        ring_ref[tile, p] = (
            total[at : at + rows]
            + total[at + rows : at + 2 * rows]
            + total[at + 2 * rows : at + 3 * rows]
        )

    sister = tile + 1 - 2 * lax.rem(tile, 2)

    def hand(block, target, index):
        return pltpu.make_async_remote_copy(
            src_ref=ring_ref.at[block],
            dst_ref=ring_ref.at[block],
            send_sem=pass_sem.at[index],
            recv_sem=ring_sem.at[block],
            device_id={"tile": target},
            device_id_type=MESH,
        )

    steps = tiles // 2
    hand(tile, sister, 0).start()
    for i in range(1, steps):
        hand(tile, lax.rem(tile + 2 * i, tiles), i).start()
    for i in range(1, steps):
        block = lax.rem(tile + tiles - 2 * i, tiles)
        hand(block, sister, 0).wait_recv()
        hand(block, sister, steps + i).start()
    hand(sister, sister, 0).wait_recv()
    for i in range(1, steps):
        hand(lax.rem(sister + tiles - 2 * i, tiles), sister, 0).wait_recv()
    out_ref[...] = ring_ref[...]
    hand(tile, sister, 0).wait_send()
    for i in range(1, steps):
        hand(tile, lax.rem(tile + 2 * i, tiles), i).wait_send()
        hand(tile, sister, steps + i).wait_send()

    @pl.loop(1, devices)
    def _(i):
        post(mine, lax.rem(mine + i, devices)).wait_send()


def spread(re, im, leads_cos, leads_sin):
    half = len(leads_cos)
    low, high = [], []
    for cos_l, sin_l in zip(leads_cos, leads_sin):
        a, b = re * cos_l, im * sin_l
        c, d = im * cos_l, re * sin_l
        high.append((a - b, c + d))
        low.append((a + b, c - d))
    assert len(low) == half
    return low[::-1] + high


def grid_kernel(windows, columns, count_ref, first_ref, vis_ref, out_ref, table_ref, hot_ref, near_ref, lead_ref):
    tile, window = pl.program_id(0), pl.program_id(1)
    blocks = vis_ref.shape[2]
    tops = columns // BLOCK
    number = count_ref[tile, window]
    lowest = (window * WINDOW).astype(jnp.float32)
    base = first_ref[0] + (tops - 1) * (BLOCK // 2) + 28
    eight = lax.broadcasted_iota(jnp.int32, (8, LANES), 0)
    start_at = (eight + base).astype(jnp.float32)
    lead_at = jnp.where(eight < 4, 4 + 8 * eight, 32 + 64 * (eight - 4)).astype(jnp.float32)
    lane = lax.broadcasted_iota(jnp.int32, (WINDOW, LANES), 0).astype(jnp.float32)

    def build(group, row):
        part = slice(group * LANES, (group + 1) * LANES)
        vis_re = vis_ref[0, 0, pl.ds(row, 1), :]
        vis_im = vis_ref[0, 1, pl.ds(row, 1), :]
        encoded = vis_ref[0, 2, pl.ds(row, 1), :] - 1.0
        line = jnp.floor(encoded * (1.0 / G))
        unit = (encoded - line * G) * (1.0 / G)
        hot_ref[group] = jnp.where(lane == line - lowest, 1.0, 0.0).astype(jnp.bfloat16)
        start_cos, start_sin = turn(start_at * unit)
        lead_cos, lead_sin = turn(lead_at * unit)
        first_re = vis_re * start_cos - vis_im * start_sin
        first_im = vis_re * start_sin + vis_im * start_cos
        small = spread(
            first_re,
            first_im,
            [lead_cos[i : i + 1] for i in range(4)],
            [lead_sin[i : i + 1] for i in range(4)],
        )
        for i, (re, im) in enumerate(small):
            near_ref[0, 8 * i : 8 * i + 8, part] = re
            near_ref[1, 8 * i : 8 * i + 8, part] = im
        lead_ref[0, :, part] = lead_cos
        lead_ref[1, :, part] = lead_sin

    def widen(group):
        part = slice(group * LANES, (group + 1) * LANES)
        for i in range(tops // 2):
            cos_l = lead_ref[0, 4 + i : 5 + i, part]
            sin_l = lead_ref[1, 4 + i : 5 + i, part]
            for lines in range(0, BLOCK, 16):
                re = near_ref[0, lines : lines + 16, part]
                im = near_ref[1, lines : lines + 16, part]
                a, b = re * cos_l, im * sin_l
                c, d = im * cos_l, re * sin_l
                at = (i * BLOCK + lines) * 4
                for n, value in enumerate((a - b, a + b, c + d, c - d)):
                    table_ref[group, at + 16 * n : at + 16 * n + 16, :] = value.astype(
                        jnp.bfloat16
                    )

    def deliver(product, add):
        for i in range(tops // 2):
            for lines in range(0, BLOCK, 16):
                high = (tops // 2 + i) * BLOCK + lines
                low = (tops // 2 - 1 - i) * BLOCK + lines
                at = (i * BLOCK + lines) * 4
                for n, row in enumerate((high, low, columns + high, columns + low)):
                    value = product[at + 16 * n : at + 16 * n + 16]
                    if add:
                        value = value + out_ref[0, row : row + 16]
                    out_ref[0, row : row + 16] = value

    def chunk(row, width, add):
        for group in range(width // LANES):
            build(group, row + group)
        for group in range(width // LANES):
            widen(group)
        groups = range(width // LANES)
        left = jnp.concatenate([table_ref[group] for group in groups], axis=1)
        right = jnp.concatenate([hot_ref[group] for group in groups], axis=1)
        deliver(lax.dot_general(left, right, NT, preferred_element_type=jnp.float32), add)

    def place(done, width):
        return jnp.where(window == 0, done, blocks - done - width // LANES)

    @pl.when(number <= NARROW)
    def _():
        chunk(place(0, NARROW), NARROW, False)

    @pl.when((number > NARROW) & (number <= HALF))
    def _():
        chunk(place(0, HALF), HALF, False)

    @pl.when((number > HALF) & (number <= HALF + NARROW))
    def _():
        chunk(place(0, HALF + NARROW), HALF + NARROW, False)

    @pl.when(number > HALF + NARROW)
    def _():
        chunk(place(0, WIDE), WIDE, False)

    rest = jnp.maximum(number - WIDE, 0)
    full = rest // WIDE
    tail = rest - full * WIDE
    full = full + jnp.where(tail > HALF, 1, 0)

    @pl.loop(0, full)
    def _(index):
        chunk(place((index + 1) * (WIDE // LANES), WIDE), WIDE, True)

    done = (full + 1) * (WIDE // LANES)

    @pl.when((tail > NARROW) & (tail <= HALF))
    def _():
        chunk(place(done, HALF), HALF, True)

    @pl.when((tail > 0) & (tail <= NARROW))
    def _():
        chunk(place(done, NARROW), NARROW, True)


def place(lane, first, second, count):
    return lax.rem(jnp.where(lane < count, first * count + lane, second * count + lane - count), WINDOW)


def squared(index):
    cosine = jnp.where(index >= G // 2, index - G, index).astype(jnp.float32) * (0.5 / G)
    return cosine * cosine


def response(taps, index):
    real = imag = None
    for j, tap in enumerate(taps):
        cos_j, sin_j = turn((index * j).astype(jnp.float32) * (1.0 / G))
        real = tap * cos_j if real is None else real + tap * cos_j
        imag = tap * sin_j if imag is None else imag + tap * sin_j
    return jnp.arctan2(imag, real) * (0.5 / math.pi), jnp.sqrt(real * real + imag * imag)


def quarter(value, turns):
    re, im = value
    return ((re, im), (-im, re), (-re, -im), (im, -re))[turns % 4]


def plus(left, right):
    return left[0] + right[0], left[1] + right[1]


def minus(left, right):
    return left[0] - right[0], left[1] - right[1]


def image_kernel(held, own, columns, scale, taps_ref, w_ref, twist_ref, *refs):
    grids, own_ref, got_ref = refs[:held], refs[held], refs[held + 1]
    mixed_ref, even_ref, odd_ref, send_ref, weight_ref, line_ref, side_ref = refs[held + 2 : -2]
    send_sem, got_sem = refs[-2:]
    width = line_ref.shape[2]
    step = pl.program_id(0)
    steps = pl.num_programs(0)
    mine = lax.axis_index("plane")
    core = lax.rem(lax.axis_index("tile"), 2)
    near = mine + 1 - 2 * lax.rem(mine, 2)
    far = mine + 2 - 4 * lax.rem(mine // 2, 2)
    partner = near * (1 - core) + far * core
    barrier = pltpu.get_barrier_semaphore()

    @pl.when(step == 0)
    def _():
        pl.semaphore_signal(
            barrier, inc=1, device_id={"plane": partner}, device_id_type=MESH
        )
        lane = lax.broadcasted_iota(jnp.int32, (DIGITS, width), 1)
        digit = lax.broadcasted_iota(jnp.int32, (DIGITS, width), 0)
        index = place(lane, partner, mine, own) * DIGITS + digit
        taps = [taps_ref[j] for j in range(taps_ref.shape[0])]
        angle, size = response(taps, index)
        line_ref[0] = 1.0 - squared(index)
        line_ref[1] = angle
        line_ref[2] = size * scale

        @pl.loop(0, WINDOW // 16)
        def _(i):
            at = pl.multiple_of(i * 16, 16)
            lane = lax.broadcasted_iota(jnp.int32, (16, width), 1)
            inner = lax.broadcasted_iota(jnp.int32, (16, width), 0) + at
            product = inner * place(lane, partner, mine, own)
            cos_d, sin_d = turn(product.astype(jnp.float32) * (1.0 / WINDOW))
            weight_ref[pl.ds(at, 16), :width] = cos_d.astype(jnp.bfloat16)
            weight_ref[pl.ds(at, 16), width:] = sin_d.astype(jnp.bfloat16)
            weight_ref[pl.ds(WINDOW + at, 16), :width] = (-sin_d).astype(jnp.bfloat16)
            weight_ref[pl.ds(WINDOW + at, 16), width:] = cos_d.astype(jnp.bfloat16)

        pl.semaphore_wait(barrier, 1)

    index = lax.axis_index("tile") * columns + step * LANES
    index = index + lax.broadcasted_iota(jnp.int32, (8, LANES), 1)
    taps = [
        jnp.full((8, LANES), taps_ref[j], jnp.float32).astype(jnp.bfloat16).astype(jnp.float32)
        for j in range(taps_ref.shape[0])
    ]
    angle, size = response(taps, index)
    for n, value in enumerate((squared(index), angle, size)):
        side_ref[n] = jnp.broadcast_to(value[0:1], (LANES, LANES)).T

    for k in range(held):
        grid_ref = grids[k]

        @pl.loop(0, LANES // 16)
        def _(index):
            at = pl.multiple_of(index * 16, 16)
            part = pl.ds(at, 16)
            for half in range(WINDOW // LANES):
                lanes = slice(half * LANES, (half + 1) * LANES)
                for b0 in range(4):
                    heads = []
                    for w0 in range(4):
                        total = None
                        for w1 in range(4):
                            w = 4 * w1 + w0
                            value = quarter(
                                (grid_ref[w, 0, part, lanes], grid_ref[w, 1, part, lanes]), w1 * b0
                            )
                            total = value if total is None else plus(total, value)
                        if w0 * b0:
                            angle = 2.0 * math.pi * w0 * b0 / DIGITS
                            c, s = math.cos(angle), math.sin(angle)
                            re, im = total
                            total = (re * c - im * s, re * s + im * c)
                        heads.append(total)
                    even, odd = plus(heads[0], heads[2]), minus(heads[0], heads[2])
                    even2, odd2 = plus(heads[1], heads[3]), minus(heads[1], heads[3])
                    odd2 = quarter(odd2, 1)
                    results = (plus(even, even2), plus(odd, odd2), minus(even, even2), minus(odd, odd2))
                    for b1, (re, im) in enumerate(results):
                        b = b0 + 4 * b1
                        if b:
                            c = twist_ref[0, b : b + 1, lanes]
                            s = twist_ref[1, b : b + 1, lanes]
                            re, im = re * c - im * s, re * s + im * c
                        rows = pl.ds(k * LANES + at, 16)
                        mixed_ref[b, half, rows, :] = re.astype(jnp.bfloat16)
                        mixed_ref[b, 2 + half, rows, :] = im.astype(jnp.bfloat16)

    def spectrum(b, full_ref):
        mixed = jnp.concatenate([mixed_ref[b, part] for part in range(4)], axis=1)
        full_ref[...] = jnp.dot(mixed, weight_ref[...], preferred_element_type=jnp.float32)

    def screen(b, full_ref):
        square = line_ref[0, pl.ds(b, 1), :] - side_ref[0]
        angle = line_ref[1, pl.ds(b, 1), :] + side_ref[1]
        drop = square * lax.rsqrt(square) - 1.0
        picture = None
        for k in range(held):
            rows = slice(k * LANES, (k + 1) * LANES)
            cos_s, sin_s = turn(w_ref[k : k + 1, :] * drop + angle, SHORT_COS, SHORT_SIN)
            value = cos_s * full_ref[rows, :width] - sin_s * full_ref[rows, width:]
            picture = value if picture is None else picture + value
        picture = (picture * (line_ref[2, pl.ds(b, 1), :] * side_ref[2])).T
        send_ref[step, b] = picture[:own]
        own_ref[0, b] = picture[own : 2 * own]

    def copy(index, piece):
        lines = pl.ds(piece * PIECE, PIECE)
        return pltpu.make_async_remote_copy(
            src_ref=send_ref.at[index, lines],
            dst_ref=got_ref.at[index, lines],
            send_sem=send_sem.at[index, piece],
            recv_sem=got_sem.at[index, piece],
            device_id={"plane": partner},
            device_id_type=MESH,
        )

    spectrum(0, even_ref)

    @pl.loop(0, DIGITS // PIECE)
    def _(piece):
        for pair in range(PIECE // 2):
            b = piece * PIECE + pair * 2
            spectrum(b + 1, odd_ref)
            screen(b, even_ref)
            spectrum(lax.rem(b + 2, DIGITS), even_ref)
            screen(b + 1, odd_ref)
        copy(step, piece).start()

    @pl.when(step == steps - 1)
    def _():
        for index in range(send_ref.shape[0]):
            for piece in range(DIGITS // PIECE):
                copy(index, piece).wait()


def sum_kernel(own_ref, got_ref, out_ref):
    for b in range(DIGITS):
        out_ref[:, b, :] = own_ref[0, b] + got_ref[0, b]


def local(visibility, target, offset, taps, w_plane):
    tiles = lax.axis_size("tile")
    planes = lax.axis_size("plane")
    devices = tiles * planes
    vis_dev = visibility.shape[1]
    capacity = 2 * vis_dev // devices
    slots = devices * capacity
    blocks = slots // LANES
    band = G // tiles
    columns = G // tiles
    windows = band // WINDOW
    own = G // planes // DIGITS
    width = max(LANES, 2 * own)
    held = planes // 2
    assert windows in (1, 2)
    vmem = pl.BlockSpec(memory_space=pltpu.VMEM)
    smem = pl.BlockSpec(memory_space=pltpu.SMEM)

    numbers = range(planes)
    jumps = [[d for d in numbers if not d & bit] for bit in (1, 2)]
    gathered, level = pl.pallas_call(
        functools.partial(front_kernel, windows, tiles, jumps),
        out_shape=[
            jax.ShapeDtypeStruct((tiles, 3, blocks, LANES), jnp.float32),
            jax.ShapeDtypeStruct((held, LANES), jnp.float32),
        ],
        in_specs=[vmem] * 3 + [smem],
        out_specs=[vmem] * 2,
        scratch_shapes=[
            pltpu.VMEM((9 * devices, vis_dev), jnp.bfloat16),
            pltpu.VMEM((LANES, vis_dev), jnp.bfloat16),
            pltpu.VMEM((9 * blocks, devices * LANES), jnp.bfloat16),
            pltpu.VMEM((LANES, devices * LANES), jnp.bfloat16),
            pltpu.VMEM((devices, 4, LANES), jnp.float32),
            pltpu.VMEM((devices, 4, LANES), jnp.float32),
            pltpu.VMEM((tiles, 3, blocks, LANES), jnp.float32),
            pltpu.SemaphoreType.DMA((devices,)),
            pltpu.SemaphoreType.DMA((devices,)),
            pltpu.SemaphoreType.DMA((tiles,)),
            pltpu.SemaphoreType.DMA((tiles,)),
        ],
        compiler_params=pltpu.CompilerParams(collective_id=1, has_side_effects=True),
    )(
        visibility.reshape(2, -1, LANES),
        target.reshape(-1, LANES),
        offset.reshape(-1, LANES),
        w_plane,
    )

    first = (lax.axis_index("tile") * columns).astype(jnp.int32)
    lists = [gathered]
    for k in range(1, held):
        moves = []
        for q in range(planes):
            for t in range(tiles):
                moves.append((q * tiles + t, (q ^ jumps[t % 2][k]) * tiles + t))
        lists.append(lax.ppermute(gathered, ("plane", "tile"), moves))

    def transform(slots_of):
        line = jnp.floor((slots_of[:, 2] - 1.0) * (1.0 / G))
        counts = jnp.stack(
            [
                jnp.sum(
                    ((line >= w * WINDOW) & (line < (w + 1) * WINDOW)).astype(jnp.int32),
                    axis=(1, 2),
                )
                for w in range(windows)
            ],
            axis=1,
        )
        return pl.pallas_call(
            functools.partial(grid_kernel, windows, columns),
            grid=(tiles, windows),
            out_shape=jax.ShapeDtypeStruct((DIGITS, 2 * columns, WINDOW), jnp.float32),
            in_specs=[
                smem,
                smem,
                pl.BlockSpec((1, 3, blocks, LANES), lambda t, w: (t, 0, 0, 0)),
            ],
            out_specs=pl.BlockSpec(
                (1, 2 * columns, WINDOW), lambda t, w: (t * windows + w, 0, 0)
            ),
            scratch_shapes=[
                pltpu.VMEM((WIDE // LANES, 2 * columns, LANES), jnp.bfloat16),
                pltpu.VMEM((WIDE // LANES, WINDOW, LANES), jnp.bfloat16),
                pltpu.VMEM((2, BLOCK, WIDE), jnp.float32),
                pltpu.VMEM((2, 8, WIDE), jnp.float32),
            ],
            cost_estimate=pl.CostEstimate(
                flops=2 * slots * tiles * columns * WINDOW, bytes_accessed=1 << 24, transcendentals=0
            ),
        )(counts, first[None], slots_of).reshape(DIGITS, 2, columns, WINDOW)

    grids = [transform(v) for v in lists]

    digits = np.arange(DIGITS)
    angles = 2.0 * np.pi * (digits[:, None] * np.arange(WINDOW)[None, :]) / G
    twist = jnp.asarray(np.stack([np.cos(angles), np.sin(angles)]).astype(np.float32))
    steps = columns // LANES
    mine_part, other_part = pl.pallas_call(
        functools.partial(image_kernel, held, own, columns, 1.0 / math.sqrt(vis_dev * devices)),
        grid=(steps,),
        out_shape=[jax.ShapeDtypeStruct((steps, DIGITS, own, LANES), jnp.float32)] * 2,
        in_specs=[
            smem,
            vmem,
            vmem,
        ]
        + [pl.BlockSpec((DIGITS, 2, LANES, WINDOW), lambda j: (0, 0, j, 0))] * held,
        out_specs=[
            pl.BlockSpec((1, DIGITS, own, LANES), lambda j: (j, 0, 0, 0)),
            pl.BlockSpec(memory_space=pl.ANY),
        ],
        scratch_shapes=[
            pltpu.VMEM((DIGITS, 4, held * LANES, LANES), jnp.bfloat16),
            pltpu.VMEM((held * LANES, 2 * width), jnp.float32),
            pltpu.VMEM((held * LANES, 2 * width), jnp.float32),
            pltpu.VMEM((steps, DIGITS, own, LANES), jnp.float32),
            pltpu.VMEM((2 * WINDOW, 2 * width), jnp.bfloat16),
            pltpu.VMEM((3, DIGITS, width), jnp.float32),
            pltpu.VMEM((3, LANES, LANES), jnp.float32),
            pltpu.SemaphoreType.DMA((steps, DIGITS // PIECE)),
            pltpu.SemaphoreType.DMA((steps, DIGITS // PIECE)),
        ],
        compiler_params=pltpu.CompilerParams(
            collective_id=0,
            has_side_effects=True,
            vmem_limit_bytes=60 * 1024 * 1024,
            dimension_semantics=("arbitrary",),
        ),
    )(taps, level, twist, *grids)
    block = pl.BlockSpec((1, DIGITS, own, LANES), lambda j: (j, 0, 0, 0))
    image = pl.pallas_call(
        sum_kernel,
        grid=(steps,),
        out_shape=jax.ShapeDtypeStruct((own, DIGITS, columns), jnp.float32),
        in_specs=[block, block],
        out_specs=pl.BlockSpec((own, DIGITS, LANES), lambda j: (0, 0, j)),
    )(mine_part, other_part)
    return image.reshape(own * DIGITS, columns)


def solution(mesh):
    return jax.shard_map(
        local,
        mesh=mesh,
        in_specs=(
            P(None, ("plane", "tile")),
            P(("plane", "tile"), None),
            P(("plane", "tile")),
            P(),
            P("plane"),
        ),
        out_specs=P("plane", "tile"),
        check_vma=False,
    )
```

profile of v0, /device:TPU:0, one launch (start us, length us, event | category | flops | bytes accessed | tf_op | source)
XLA Modules:
  0.0 117.8 jit_solution(17863614692622511210)
XLA Ops:
  0.7 1.3 %copy.15 = f32[1,2,16,128]{3,2,1,0:T(8,128)} copy(f32[1,2,16,128]{3,1,2,0:T(2,128)} %bitcast.17) | data formatting | bytes 32768
  2.0 21.6 %shard_map.64 = (f32[8,3,32,128]{3,2,1,0:T(8,128)}, f32[2,128]{1,0:T(2,128)}) custom-call(f32[2,16,128]{2,1,0:T(8,128)} %bitcast.16, s32[16,128]{1,0:T(8,128)} %bitcast.18, s32[16,128]{1,0:T(8,128)} %bitcast.19, f32[1]{0:T(128)S(6)} %copy.16.w_ref), custom_call_target="tpu_custom_call" | custom-call | tf_op jit(solution)/shard_map/pallas_call | solution.py:556
  23.6 1.4 %collective-permute-start = (f32[8,3,32,128]{3,2,1,0:T(8,128)}, f32[8,3,32,128]{3,2,1,0:T(8,128)S(1)}, u32[]{:S(2)}, u32[]{:S(2)}) collective-permute-start(f32[8,3,32,128]{3,2,1,0:T(8,128)} %get-tuple-element.10.vis_ref), channel_id=1, source_target_pairs={{0,16},{1,9},{2,18},{3,11},{4,20},{5,13},{6,22},{7,15},{8,24},{9,1... | collective-permute-start | bytes 1179656 | tf_op jit(solution)/shard_map/ppermute | solution.py:592
  25.0 1.3 %convert_reduce_fusion.3 = (s32[8]{0:T(128)S(1)}, s32[8]{0:T(128)S(1)}) fusion(f32[8,3,32,128]{3,2,1,0:T(8,128)} %get-tuple-element.10.vis_ref), kind=kLoop, calls=%fused_computation.6 | loop fusion | flops 425968 | bytes 131136 | tf_op jit(solution)/shard_map/reduce_sum | solution.py:598
  26.3 0.7 copy.11.count_ref
  27.0 23.5 %shard_map.65 = f32[16,1024,256]{2,1,0:T(8,128)} custom-call(s32[8,2]{1,0:T(8,128)} %copy.11.count_ref, s32[1]{0:T(128)} %bitcast.4.first_ref, f32[8,3,32,128]{3,2,1,0:T(8,128)} %get-tuple-element.10.vis_ref), custom_call_target="tpu_custom_call" | custom-call | flops 8589934592 | bytes 16777216 | tf_op jit(solution)/shard_map/pallas_call | solution.py:606
  50.5 0.0 collective-permute-done.vis_ref
  50.5 0.0 copy-start
  50.5 0.4 convert_reduce_fusion.1
  50.9 0.7 copy.12.count_ref
  51.5 0.0 copy-done
  51.5 21.3 %shard_map.66 = f32[16,1024,256]{2,1,0:T(8,128)} custom-call(s32[8,2]{1,0:T(8,128)} %copy.12.count_ref, s32[1]{0:T(128)} %bitcast.4.first_ref, f32[8,3,32,128]{3,2,1,0:T(8,128)} %copy-done), custom_call_target="tpu_custom_call" | custom-call | flops 8589934592 | bytes 16777216 | tf_op jit(solution)/shard_map/pallas_call | solution.py:606
  72.8 40.2 %shard_map.67 = (f32[4,16,64,128]{3,2,1,0:T(8,128)}, f32[4,16,64,128]{3,2,1,0:T(8,128)}) custom-call(f32[8]{0:T(128)} %taps_ref.1, f32[2,128]{1,0:T(2,128)} %get-tuple-element.9.w_ref, f32[2,16,256]{2,1,0:T(8,128)} %constant.22.clone.twist_ref, f32[16,2,512,256]{3,2,1,0:T(8,128)} %bitcast.14, f32[16,2,512,256]{3,2,1,0:T(8,128)} %bitcast.15), custom_call_target="tpu_custom_call" | custom-call | tf_op jit(solution)/shard_map/pallas_call | solution.py:635
  113.1 4.7 %shard_map.68 = f32[64,16,512]{2,1,0:T(8,128)} custom-call(f32[4,16,64,128]{3,2,1,0:T(8,128)} %get-tuple-element.11.own_ref, f32[4,16,64,128]{3,2,1,0:T(8,128)} %get-tuple-element.12.got_ref), custom_call_target="tpu_custom_call" | custom-call | tf_op jit(solution)/shard_map/pallas_call | solution.py:668
  (2 shorter events, 0.0 us)
Async XLA Ops:
  23.6 26.9 %collective-permute-start = (f32[8,3,32,128]{3,2,1,0:T(8,128)}, f32[8,3,32,128]{3,2,1,0:T(8,128)S(1)}, u32[]{:S(2)}, u32[]{:S(2)}) collective-permute-start(f32[8,3,32,128]{3,2,1,0:T(8,128)} %get-tuple-element.10.vis_ref), channel_id=1, source_target_pairs={{0,16},{1,9},{2,18},{3,11},{4,20},{5,13},{6,22},{7,15},{8,24},{9,1... | collective-permute-start | bytes 1179656 | tf_op jit(solution)/shard_map/ppermute | solution.py:592
  50.5 1.1 copy-start
where the time goes:
time: 118 us
  Pallas kernels  111 us (94%)
  local copies, waits for them, and re-layouts  2.69 us (2%)
  other arithmetic  1.74 us (1%)
  starting transfers between devices  1.36 us (1%)
    pallas_call x2, Pallas kernels, transform(): pl.pallas_call(functools.partial(grid_kernel, windows, columns), grid=(ti...  44.8 us
    pallas_call x1, Pallas kernels, local(): pl.pallas_call(functools.partial(image_kernel, held, own, columns, 1.0 /...  40.2 us
    pallas_call x1, Pallas kernels, local(): pl.pallas_call(functools.partial(front_kernel, windows, tiles, jumps), ou...  21.6 us
    pallas_call x1, Pallas kernels, local(): pl.pallas_call(sum_kernel, grid=(steps,), out_shape=jax.ShapeDtypeStruct(...  4.74 us
  transfers between devices with their start and end apart: 1, of which 0 were waited for; matrix products, arithmetic and copies ran while one was open for 2% of the time, Pallas kernels for 20%

commit v1 on v0

--- a/solution.py
+++ b/solution.py
@@ -111,8 +111,8 @@
         carry = carry + jnp.sum(hot, axis=1, keepdims=True)
         rhs_ref[:, part] = jnp.where(slot == rank, 1.0, 0.0).astype(jnp.bfloat16)
         rows = (
-            vis_ref[0, k : k + 1, :],
-            vis_ref[1, k : k + 1, :],
+            vis_ref[0:1, part],
+            vis_ref[1:2, part],
             offset_ref[k : k + 1, :].astype(jnp.float32) + 1.0,
         )
         for p, row in enumerate(rows):
@@ -155,7 +155,7 @@
         origin = (near * (1 - core) + far * core) * tiles + tile
         level_ref[k : k + 1, :] = got_ref[origin, 3:4, :]
 
-    rows = out_ref.shape[2]
+    rows = left_ref.shape[0] // 9
     encoded = got_ref[:, 2, :]
     row = jnp.floor((encoded - 1.0) * (1.0 / G))
     lower = jnp.where(
@@ -173,6 +173,8 @@
             jnp.dot(lower, flags, preferred_element_type=jnp.float32), axis=1, keepdims=True
         )
         place = inside + ahead
+        number = jnp.sum(jnp.sum(member, axis=1, keepdims=True), axis=0, keepdims=True)
+        ring_ref[tile, 3 * rows + w : 3 * rows + w + 1] = jnp.broadcast_to(number, (1, LANES))
         if w == 1:
             place = rows * LANES - 1 - place
         position = jnp.where(member > 0.0, place, position)
@@ -193,12 +195,13 @@
     total = lax.dot_general(left_ref[...], right_ref[...], NT, preferred_element_type=jnp.float32)
     for p in range(3):
         at = p * 3 * rows
-        ring_ref[tile, p] = (
+        ring_ref[tile, p * rows : (p + 1) * rows] = (
             total[at : at + rows]
             + total[at + rows : at + 2 * rows]
             + total[at + 2 * rows : at + 3 * rows]
         )
 
+    ring_ref[tile, 3 * rows + windows :] = jnp.zeros((8 - windows, LANES), jnp.float32)
     sister = tile + 1 - 2 * lax.rem(tile, 2)
 
     def hand(block, target, index):
@@ -245,26 +248,53 @@
     return low[::-1] + high
 
 
-def grid_kernel(windows, columns, count_ref, first_ref, vis_ref, out_ref, table_ref, hot_ref, near_ref, lead_ref):
-    tile, window = pl.program_id(0), pl.program_id(1)
-    blocks = vis_ref.shape[2]
+def grid_kernel(
+    windows, columns, vis_ref, grid_ref, table_ref, hot_ref, near_ref, lead_ref, sum_ref, done_sem
+):
+    tiles = vis_ref.shape[0]
+    blocks = (vis_ref.shape[1] - 8) // 3
     tops = columns // BLOCK
-    number = count_ref[tile, window]
-    lowest = (window * WINDOW).astype(jnp.float32)
-    base = first_ref[0] + (tops - 1) * (BLOCK // 2) + 28
+    base = lax.axis_index("tile") * columns + (tops - 1) * (BLOCK // 2) + 28
     eight = lax.broadcasted_iota(jnp.int32, (8, LANES), 0)
     start_at = (eight + base).astype(jnp.float32)
     lead_at = jnp.where(eight < 4, 4 + 8 * eight, 32 + 64 * (eight - 4)).astype(jnp.float32)
     lane = lax.broadcasted_iota(jnp.int32, (WINDOW, LANES), 0).astype(jnp.float32)
 
+    def drain(item):
+        slot = lax.rem(item, 2)
+        return pltpu.make_async_copy(sum_ref.at[slot], grid_ref.at[item], done_sem.at[slot])
+
+    @pl.loop(0, tiles * windows)
+    def _(item):
+        tile, window = item // windows, lax.rem(item, windows)
+
+        @pl.when(item >= 2)
+        def _():
+            drain(item - 2).wait()
+
+        fill(tile, window, blocks, tops, columns, start_at, lead_at, lane,
+             vis_ref, sum_ref.at[lax.rem(item, 2)], table_ref, hot_ref, near_ref, lead_ref)
+        drain(item).start()
+
+    for item in range(max(0, tiles * windows - 2), tiles * windows):
+        drain(item).wait()
+
+
+def fill(
+    tile, window, blocks, tops, columns, start_at, lead_at, lane,
+    vis_ref, out_ref, table_ref, hot_ref, near_ref, lead_ref,
+):
+    number = vis_ref[tile, pl.ds(3 * blocks + window, 1), :][0, 0].astype(jnp.int32)
+    lowest = (window * WINDOW).astype(jnp.float32)
+
     def build(group, row):
         part = slice(group * LANES, (group + 1) * LANES)
-        vis_re = vis_ref[0, 0, pl.ds(row, 1), :]
-        vis_im = vis_ref[0, 1, pl.ds(row, 1), :]
-        encoded = vis_ref[0, 2, pl.ds(row, 1), :] - 1.0
+        vis_re = vis_ref[tile, pl.ds(row, 1), :]
+        vis_im = vis_ref[tile, pl.ds(blocks + row, 1), :]
+        encoded = vis_ref[tile, pl.ds(2 * blocks + row, 1), :] - 1.0
         line = jnp.floor(encoded * (1.0 / G))
         unit = (encoded - line * G) * (1.0 / G)
-        hot_ref[group] = jnp.where(lane == line - lowest, 1.0, 0.0).astype(jnp.bfloat16)
+        hot_ref[group, :WINDOW] = jnp.where(lane == line - lowest, 1.0, 0.0).astype(jnp.bfloat16)
         start_cos, start_sin = turn(start_at * unit)
         lead_cos, lead_sin = turn(lead_at * unit)
         first_re = vis_re * start_cos - vis_im * start_sin
@@ -306,8 +336,8 @@
                 for n, row in enumerate((high, low, columns + high, columns + low)):
                     value = product[at + 16 * n : at + 16 * n + 16]
                     if add:
-                        value = value + out_ref[0, row : row + 16]
-                    out_ref[0, row : row + 16] = value
+                        value = value + out_ref[row : row + 16]
+                    out_ref[row : row + 16] = value
 
     def chunk(row, width, add):
         for group in range(width // LANES):
@@ -315,8 +345,8 @@
         for group in range(width // LANES):
             widen(group)
         groups = range(width // LANES)
-        left = jnp.concatenate([table_ref[group] for group in groups], axis=1)
-        right = jnp.concatenate([hot_ref[group] for group in groups], axis=1)
+        left = jnp.concatenate([table_ref[group, : 2 * columns] for group in groups], axis=1)
+        right = jnp.concatenate([hot_ref[group, :WINDOW] for group in groups], axis=1)
         deliver(lax.dot_general(left, right, NT, preferred_element_type=jnp.float32), add)
 
     def place(done, width):
@@ -381,6 +411,19 @@
     return ((re, im), (-im, re), (-re, -im), (im, -re))[turns % 4]
 
 
+def rotate(value, sixteenths):
+    value = quarter(value, sixteenths // 4)
+    rest = sixteenths % 4
+    if rest == 0:
+        return value
+    re, im = value
+    if rest == 2:
+        root = math.sqrt(0.5)
+        return (re - im) * root, (re + im) * root
+    c, s = math.cos(rest * math.pi / 8), math.sin(rest * math.pi / 8)
+    return re * c - im * s, re * s + im * c
+
+
 def plus(left, right):
     return left[0] + right[0], left[1] + right[1]
 
@@ -389,10 +432,10 @@
     return left[0] - right[0], left[1] - right[1]
 
 
-def image_kernel(held, own, columns, scale, taps_ref, w_ref, twist_ref, *refs):
+def image_kernel(held, own, columns, scale, taps_ref, w_ref, *refs):
     grids, own_ref, got_ref = refs[:held], refs[held], refs[held + 1]
-    mixed_ref, even_ref, odd_ref, send_ref, weight_ref, line_ref, side_ref = refs[held + 2 : -2]
-    send_sem, got_sem = refs[-2:]
+    mixed_ref, even_ref, odd_ref, send_ref, weight_ref, line_ref, side_ref = refs[held + 2 : -4]
+    held_ref, send_sem, got_sem, load_sem = refs[-4:]
     width = line_ref.shape[2]
     step = pl.program_id(0)
     steps = pl.num_programs(0)
@@ -403,6 +446,23 @@
     partner = near * (1 - core) + far * core
     barrier = pltpu.get_barrier_semaphore()
 
+    def fetch(index, k):
+        slot = lax.rem(index, 2)
+        lines = pl.ds(pl.multiple_of(index * LANES, LANES), LANES)
+        return pltpu.make_async_copy(
+            grids[k].at[:, :, lines, :], held_ref.at[slot, k], load_sem.at[slot, k]
+        )
+
+    @pl.when(step == 0)
+    def _():
+        for k in range(held):
+            fetch(step, k).start()
+
+    @pl.when(step < steps - 1)
+    def _():
+        for k in range(held):
+            fetch(step + 1, k).start()
+
     @pl.when(step == 0)
     def _():
         pl.semaphore_signal(
@@ -424,10 +484,15 @@
             inner = lax.broadcasted_iota(jnp.int32, (16, width), 0) + at
             product = inner * place(lane, partner, mine, own)
             cos_d, sin_d = turn(product.astype(jnp.float32) * (1.0 / WINDOW))
-            weight_ref[pl.ds(at, 16), :width] = cos_d.astype(jnp.bfloat16)
-            weight_ref[pl.ds(at, 16), width:] = sin_d.astype(jnp.bfloat16)
-            weight_ref[pl.ds(WINDOW + at, 16), :width] = (-sin_d).astype(jnp.bfloat16)
-            weight_ref[pl.ds(WINDOW + at, 16), width:] = cos_d.astype(jnp.bfloat16)
+            cos_s, sin_s = turn(inner.astype(jnp.float32) * (1.0 / G))
+            upper, under = pl.ds(at, 16), pl.ds(WINDOW + at, 16)
+            for b in range(DIGITS):
+                real = cos_d.astype(jnp.bfloat16)
+                weight_ref[b, 0, upper, :] = real
+                weight_ref[b, 1, upper, :] = sin_d.astype(jnp.bfloat16)
+                weight_ref[b, 0, under, :] = (-sin_d).astype(jnp.bfloat16)
+                weight_ref[b, 1, under, :] = real
+                cos_d, sin_d = cos_d * cos_s - sin_d * sin_s, cos_d * sin_s + sin_d * cos_s
 
         pl.semaphore_wait(barrier, 1)
 
@@ -442,7 +507,8 @@
         side_ref[n] = jnp.broadcast_to(value[0:1], (LANES, LANES)).T
 
     for k in range(held):
-        grid_ref = grids[k]
+        fetch(step, k).wait()
+        grid_ref = held_ref.at[lax.rem(step, 2), k]
 
         @pl.loop(0, LANES // 16)
         def _(index):
@@ -460,11 +526,7 @@
                                 (grid_ref[w, 0, part, lanes], grid_ref[w, 1, part, lanes]), w1 * b0
                             )
                             total = value if total is None else plus(total, value)
-                        if w0 * b0:
-                            angle = 2.0 * math.pi * w0 * b0 / DIGITS
-                            c, s = math.cos(angle), math.sin(angle)
-                            re, im = total
-                            total = (re * c - im * s, re * s + im * c)
+                        total = rotate(total, w0 * b0)
                         heads.append(total)
                     even, odd = plus(heads[0], heads[2]), minus(heads[0], heads[2])
                     even2, odd2 = plus(heads[1], heads[3]), minus(heads[1], heads[3])
@@ -472,17 +534,14 @@
                     results = (plus(even, even2), plus(odd, odd2), minus(even, even2), minus(odd, odd2))
                     for b1, (re, im) in enumerate(results):
                         b = b0 + 4 * b1
-                        if b:
-                            c = twist_ref[0, b : b + 1, lanes]
-                            s = twist_ref[1, b : b + 1, lanes]
-                            re, im = re * c - im * s, re * s + im * c
                         rows = pl.ds(k * LANES + at, 16)
                         mixed_ref[b, half, rows, :] = re.astype(jnp.bfloat16)
                         mixed_ref[b, 2 + half, rows, :] = im.astype(jnp.bfloat16)
 
     def spectrum(b, full_ref):
         mixed = jnp.concatenate([mixed_ref[b, part] for part in range(4)], axis=1)
-        full_ref[...] = jnp.dot(mixed, weight_ref[...], preferred_element_type=jnp.float32)
+        weight = jnp.concatenate([weight_ref[b, part] for part in range(2)], axis=1)
+        full_ref[...] = jnp.dot(mixed, weight, preferred_element_type=jnp.float32)
 
     def screen(b, full_ref):
         square = line_ref[0, pl.ds(b, 1), :] - side_ref[0]
@@ -529,8 +588,10 @@
 
 
 def sum_kernel(own_ref, got_ref, out_ref):
-    for b in range(DIGITS):
-        out_ref[:, b, :] = own_ref[0, b] + got_ref[0, b]
+    for index in range(own_ref.shape[0]):
+        lanes = slice(index * LANES, (index + 1) * LANES)
+        for b in range(DIGITS):
+            out_ref[:, b, lanes] = own_ref[index, b] + got_ref[index, b]
 
 
 def local(visibility, target, offset, taps, w_plane):
@@ -556,7 +617,7 @@
     gathered, level = pl.pallas_call(
         functools.partial(front_kernel, windows, tiles, jumps),
         out_shape=[
-            jax.ShapeDtypeStruct((tiles, 3, blocks, LANES), jnp.float32),
+            jax.ShapeDtypeStruct((tiles, 3 * blocks + 8, LANES), jnp.float32),
             jax.ShapeDtypeStruct((held, LANES), jnp.float32),
         ],
         in_specs=[vmem] * 3 + [smem],
@@ -568,7 +629,7 @@
             pltpu.VMEM((LANES, devices * LANES), jnp.bfloat16),
             pltpu.VMEM((devices, 4, LANES), jnp.float32),
             pltpu.VMEM((devices, 4, LANES), jnp.float32),
-            pltpu.VMEM((tiles, 3, blocks, LANES), jnp.float32),
+            pltpu.VMEM((tiles, 3 * blocks + 8, LANES), jnp.float32),
             pltpu.SemaphoreType.DMA((devices,)),
             pltpu.SemaphoreType.DMA((devices,)),
             pltpu.SemaphoreType.DMA((tiles,)),
@@ -576,13 +637,12 @@
         ],
         compiler_params=pltpu.CompilerParams(collective_id=1, has_side_effects=True),
     )(
-        visibility.reshape(2, -1, LANES),
+        visibility,
         target.reshape(-1, LANES),
         offset.reshape(-1, LANES),
         w_plane,
     )
 
-    first = (lax.axis_index("tile") * columns).astype(jnp.int32)
     lists = [gathered]
     for k in range(1, held):
         moves = []
@@ -592,45 +652,26 @@
         lists.append(lax.ppermute(gathered, ("plane", "tile"), moves))
 
     def transform(slots_of):
-        line = jnp.floor((slots_of[:, 2] - 1.0) * (1.0 / G))
-        counts = jnp.stack(
-            [
-                jnp.sum(
-                    ((line >= w * WINDOW) & (line < (w + 1) * WINDOW)).astype(jnp.int32),
-                    axis=(1, 2),
-                )
-                for w in range(windows)
-            ],
-            axis=1,
-        )
         return pl.pallas_call(
             functools.partial(grid_kernel, windows, columns),
-            grid=(tiles, windows),
             out_shape=jax.ShapeDtypeStruct((DIGITS, 2 * columns, WINDOW), jnp.float32),
-            in_specs=[
-                smem,
-                smem,
-                pl.BlockSpec((1, 3, blocks, LANES), lambda t, w: (t, 0, 0, 0)),
-            ],
-            out_specs=pl.BlockSpec(
-                (1, 2 * columns, WINDOW), lambda t, w: (t * windows + w, 0, 0)
-            ),
+            in_specs=[vmem],
+            out_specs=pl.BlockSpec(memory_space=pl.ANY),
             scratch_shapes=[
-                pltpu.VMEM((WIDE // LANES, 2 * columns, LANES), jnp.bfloat16),
-                pltpu.VMEM((WIDE // LANES, WINDOW, LANES), jnp.bfloat16),
-                pltpu.VMEM((2, BLOCK, WIDE), jnp.float32),
+                pltpu.VMEM((WIDE // LANES, 2 * columns + 16, LANES), jnp.bfloat16),
+                pltpu.VMEM((WIDE // LANES, WINDOW + 16, LANES), jnp.bfloat16),
+                pltpu.VMEM((2, BLOCK + 8, WIDE + LANES), jnp.float32),
                 pltpu.VMEM((2, 8, WIDE), jnp.float32),
+                pltpu.VMEM((2, 2 * columns, WINDOW), jnp.float32),
+                pltpu.SemaphoreType.DMA((2,)),
             ],
             cost_estimate=pl.CostEstimate(
                 flops=2 * slots * tiles * columns * WINDOW, bytes_accessed=1 << 24, transcendentals=0
             ),
-        )(counts, first[None], slots_of).reshape(DIGITS, 2, columns, WINDOW)
+        )(slots_of).reshape(DIGITS, 2, columns, WINDOW)
 
     grids = [transform(v) for v in lists]
 
-    digits = np.arange(DIGITS)
-    angles = 2.0 * np.pi * (digits[:, None] * np.arange(WINDOW)[None, :]) / G
-    twist = jnp.asarray(np.stack([np.cos(angles), np.sin(angles)]).astype(np.float32))
     steps = columns // LANES
     mine_part, other_part = pl.pallas_call(
         functools.partial(image_kernel, held, own, columns, 1.0 / math.sqrt(vis_dev * devices)),
@@ -639,9 +680,8 @@
         in_specs=[
             smem,
             vmem,
-            vmem,
         ]
-        + [pl.BlockSpec((DIGITS, 2, LANES, WINDOW), lambda j: (0, 0, j, 0))] * held,
+        + [pl.BlockSpec(memory_space=pl.ANY)] * held,
         out_specs=[
             pl.BlockSpec((1, DIGITS, own, LANES), lambda j: (j, 0, 0, 0)),
             pl.BlockSpec(memory_space=pl.ANY),
@@ -651,11 +691,13 @@
             pltpu.VMEM((held * LANES, 2 * width), jnp.float32),
             pltpu.VMEM((held * LANES, 2 * width), jnp.float32),
             pltpu.VMEM((steps, DIGITS, own, LANES), jnp.float32),
-            pltpu.VMEM((2 * WINDOW, 2 * width), jnp.bfloat16),
+            pltpu.VMEM((DIGITS, 2, 2 * WINDOW, width), jnp.bfloat16),
             pltpu.VMEM((3, DIGITS, width), jnp.float32),
             pltpu.VMEM((3, LANES, LANES), jnp.float32),
+            pltpu.VMEM((2, held, DIGITS, 2, LANES, WINDOW), jnp.float32),
             pltpu.SemaphoreType.DMA((steps, DIGITS // PIECE)),
             pltpu.SemaphoreType.DMA((steps, DIGITS // PIECE)),
+            pltpu.SemaphoreType.DMA((2, held)),
         ],
         compiler_params=pltpu.CompilerParams(
             collective_id=0,
@@ -663,14 +705,14 @@
             vmem_limit_bytes=60 * 1024 * 1024,
             dimension_semantics=("arbitrary",),
         ),
-    )(taps, level, twist, *grids)
-    block = pl.BlockSpec((1, DIGITS, own, LANES), lambda j: (j, 0, 0, 0))
+    )(taps, level, *grids)
+    block = pl.BlockSpec((steps // 2, DIGITS, own, LANES), lambda j: (j, 0, 0, 0))
     image = pl.pallas_call(
         sum_kernel,
-        grid=(steps,),
+        grid=(2,),
         out_shape=jax.ShapeDtypeStruct((own, DIGITS, columns), jnp.float32),
         in_specs=[block, block],
-        out_specs=pl.BlockSpec((own, DIGITS, LANES), lambda j: (0, 0, j)),
+        out_specs=pl.BlockSpec((own, DIGITS, columns // 2), lambda j: (0, 0, j)),
     )(mine_part, other_part)
     return image.reshape(own * DIGITS, columns)
 

time: 118 us -> 109 us (0.924)
  Pallas kernels: 111 us -> 105 us
  local copies, waits for them, and re-layouts: 2.69 us -> 0.75 us
  other arithmetic: 1.74 us -> 0 us
    pallas_call x1, Pallas kernels: 40.2 us -> 34.8 us  [local(): pl.pallas_call(functools.partial(image_kernel, held, own, columns, 1.0 /...]
    reduce_sum x2 -> x0, other arithmetic: 1.72 us -> none  [transform(): jnp.sum(((line >= w * WINDOW) & (line < (w + 1) * WINDOW)).astype(jnp.int...]
    pallas_call x3, Pallas kernels: 49.5 us -> 48.1 us  [the longest x2 43.5 us: transform(): pl.pallas_call(functools.partial(grid_kernel, windows, columns), out_shap...]
    another operation x2 -> x0, local copies, waits for them, and re-layouts: 1.36 us -> none  [transform(): jnp.stack([jnp.sum(((line >= w * WINDOW) & (line < (w + 1) * WINDOW)).ast...]
  transfers between devices with their start and end apart: 1 -> 1, of which waited for: 0 -> 0; matrix products, arithmetic and copies ran while one was open for 2% -> 0% of each run, Pallas kernels for 20% -> 21%
where the time goes in v1:
time: 109 us; the launch traced here: 108 us
  Pallas kernels  105 us (96%)
  starting transfers between devices  1.36 us (1%)
    pallas_call x2, Pallas kernels, transform(): pl.pallas_call(functools.partial(grid_kernel, windows, columns), out_shap...  43.5 us
    pallas_call x1, Pallas kernels, local(): pl.pallas_call(functools.partial(image_kernel, held, own, columns, 1.0 /...  34.8 us
    pallas_call x1, Pallas kernels, local(): pl.pallas_call(functools.partial(front_kernel, windows, tiles, jumps), ou...  22 us
    pallas_call x1, Pallas kernels, local(): pl.pallas_call(sum_kernel, grid=(2,), out_shape=jax.ShapeDtypeStruct((own...  4.67 us
  transfers between devices with their start and end apart: 1, of which 0 were waited for; matrix products, arithmetic and copies ran while one was open for 0% of the time, Pallas kernels for 21%

profile of v1, /device:TPU:0, one launch (start us, length us, event | category | flops | bytes accessed | tf_op | source)
XLA Modules:
  0.0 107.7 jit_solution(16757629749108069855)
XLA Ops:
  0.7 22.0 %shard_map.55 = (f32[8,104,128]{2,1,0:T(8,128)}, f32[2,128]{1,0:T(2,128)}) custom-call(f32[2,2048]{1,0:T(2,128)} %vis_ref.1, s32[16,128]{1,0:T(8,128)} %bitcast.7, s32[16,128]{1,0:T(8,128)} %bitcast.8, f32[1]{0:T(128)S(6)} %copy.6.w_ref), custom_call_target="tpu_custom_call" | custom-call | tf_op jit(solution)/shard_map/pallas_call | solution.py:617
  22.6 1.4 %collective-permute-start = (f32[8,104,128]{2,1,0:T(8,128)}, f32[8,104,128]{2,1,0:T(8,128)S(1)}, u32[]{:S(2)}, u32[]{:S(2)}) collective-permute-start(f32[8,104,128]{2,1,0:T(8,128)} %get-tuple-element.10.vis_ref), channel_id=1, source_target_pairs={{0,16},{1,9},{2,18},{3,11},{4,20},{5,13},{6,22},{7,15},{8,24},{9,1... | collective-permute-start | bytes 1277960 | tf_op jit(solution)/shard_map/ppermute | solution.py:652
  24.0 22.7 %shard_map.56 = f32[16,1024,256]{2,1,0:T(8,128)} custom-call(f32[8,104,128]{2,1,0:T(8,128)} %get-tuple-element.10.vis_ref), custom_call_target="tpu_custom_call" | custom-call | flops 8589934592 | bytes 16777216 | tf_op jit(solution)/shard_map/pallas_call | solution.py:655
  46.7 0.0 collective-permute-done.vis_ref
  46.7 0.0 copy-start
  46.7 0.7 copy-done
  47.5 20.8 %shard_map.57 = f32[16,1024,256]{2,1,0:T(8,128)} custom-call(f32[8,104,128]{2,1,0:T(8,128)} %copy-done), custom_call_target="tpu_custom_call" | custom-call | flops 8589934592 | bytes 16777216 | tf_op jit(solution)/shard_map/pallas_call | solution.py:655
  68.2 34.8 %shard_map.58 = (f32[4,16,64,128]{3,2,1,0:T(8,128)}, f32[4,16,64,128]{3,2,1,0:T(8,128)}) custom-call(f32[8]{0:T(128)} %taps_ref.1, f32[2,128]{1,0:T(2,128)} %get-tuple-element.9.w_ref, f32[16,2,512,256]{3,2,1,0:T(8,128)} %bitcast.5, f32[16,2,512,256]{3,2,1,0:T(8,128)} %bitcast.6), custom_call_target="tpu_custom_call" | custom-call | tf_op jit(solution)/shard_map/pallas_call | solution.py:676
  103.1 4.7 %shard_map.59 = f32[64,16,512]{2,1,0:T(8,128)} custom-call(f32[4,16,64,128]{3,2,1,0:T(8,128)} %get-tuple-element.11.own_ref, f32[4,16,64,128]{3,2,1,0:T(8,128)} %get-tuple-element.12.got_ref), custom_call_target="tpu_custom_call" | custom-call | tf_op jit(solution)/shard_map/pallas_call | solution.py:710
Async XLA Ops:
  22.6 24.1 %collective-permute-start = (f32[8,104,128]{2,1,0:T(8,128)}, f32[8,104,128]{2,1,0:T(8,128)S(1)}, u32[]{:S(2)}, u32[]{:S(2)}) collective-permute-start(f32[8,104,128]{2,1,0:T(8,128)} %get-tuple-element.10.vis_ref), channel_id=1, source_target_pairs={{0,16},{1,9},{2,18},{3,11},{4,20},{5,13},{6,22},{7,15},{8,24},{9,1... | collective-permute-start | bytes 1277960 | tf_op jit(solution)/shard_map/ppermute | solution.py:652
  46.7 0.8 copy-start

commit v2 on v1

--- a/solution.py
+++ b/solution.py
@@ -79,14 +79,22 @@
 
 
 def front_kernel(
-    windows, tiles, jumps, vis_ref, target_ref, offset_ref, w_ref, out_ref, level_ref,
-    lhs_ref, rhs_ref, left_ref, right_ref, send_ref, got_ref, ring_ref,
+    windows, tiles, jumps, vis_in, target_in, offset_in, w_ref, out_ref, level_ref,
+    vis_ref, target_ref, offset_ref, in_sem, lhs_ref, rhs_ref, left_ref, right_ref, send_ref, got_ref, ring_ref,
     send_sem, got_sem, pass_sem, ring_sem,
 ):
     devices = send_ref.shape[0]
     plane, tile = lax.axis_index("plane"), lax.axis_index("tile")
     mine = plane * tiles + tile
     barrier = pltpu.get_barrier_semaphore()
+    inputs = [
+        pltpu.make_async_copy(source, target, in_sem.at[n])
+        for n, (source, target) in enumerate(
+            ((vis_in, vis_ref), (target_in, target_ref), (offset_in, offset_ref))
+        )
+    ]
+    for copy in inputs:
+        copy.start()
 
     def seat(device):
         return {"plane": device // tiles, "tile": lax.rem(device, tiles)}
@@ -97,6 +105,8 @@
             barrier, inc=1, device_id=seat(lax.rem(mine + i, devices)), device_id_type=MESH
         )
 
+    for copy in inputs:
+        copy.wait()
     blocks = target_ref.shape[0]
     upper = strict_upper(LANES)
     line = lax.broadcasted_iota(jnp.int32, (devices, LANES), 0)
@@ -249,9 +259,18 @@
 
 
 def grid_kernel(
-    windows, columns, vis_ref, grid_ref, table_ref, hot_ref, near_ref, lead_ref, sum_ref, done_sem
+    windows, columns, list_ref, grid_ref, table_ref, hot_ref, near_ref, lead_ref, sum_ref, vis_ref,
+    done_sem, load_sem,
 ):
     tiles = vis_ref.shape[0]
+
+    def load(tile):
+        return pltpu.make_async_copy(list_ref.at[tile], vis_ref.at[tile], load_sem.at[tile])
+
+    @pl.loop(0, tiles)
+    def _(tile):
+        load(tile).start()
+
     blocks = (vis_ref.shape[1] - 8) // 3
     tops = columns // BLOCK
     base = lax.axis_index("tile") * columns + (tops - 1) * (BLOCK // 2) + 28
@@ -267,6 +286,10 @@
     @pl.loop(0, tiles * windows)
     def _(item):
         tile, window = item // windows, lax.rem(item, windows)
+
+        @pl.when(window == 0)
+        def _():
+            load(tile).wait()
 
         @pl.when(item >= 2)
         def _():
@@ -446,22 +469,29 @@
     partner = near * (1 - core) + far * core
     barrier = pltpu.get_barrier_semaphore()
 
-    def fetch(index, k):
+    def fetch(index, k, part):
         slot = lax.rem(index, 2)
-        lines = pl.ds(pl.multiple_of(index * LANES, LANES), LANES)
+        source = pl.ds(pl.multiple_of(index * LANES + part * 32, 32), 32)
+        lines = pl.ds(pl.multiple_of(part * 32, 32), 32)
         return pltpu.make_async_copy(
-            grids[k].at[:, :, lines, :], held_ref.at[slot, k], load_sem.at[slot, k]
-        )
+            grids[k].at[:, :, source, :],
+            held_ref.at[slot, k, :, :, lines, :],
+            load_sem.at[slot, k, part],
+        )
+
+    parts = LANES // 32
 
     @pl.when(step == 0)
     def _():
         for k in range(held):
-            fetch(step, k).start()
-
-    @pl.when(step < steps - 1)
+            for part in range(parts):
+                fetch(step, k, part).start()
+
+    @pl.when((step > 0) & (step < steps - 1))
     def _():
         for k in range(held):
-            fetch(step + 1, k).start()
+            for part in range(parts):
+                fetch(step + 1, k, part).start()
 
     @pl.when(step == 0)
     def _():
@@ -507,36 +537,43 @@
         side_ref[n] = jnp.broadcast_to(value[0:1], (LANES, LANES)).T
 
     for k in range(held):
-        fetch(step, k).wait()
         grid_ref = held_ref.at[lax.rem(step, 2), k]
 
-        @pl.loop(0, LANES // 16)
-        def _(index):
-            at = pl.multiple_of(index * 16, 16)
-            part = pl.ds(at, 16)
-            for half in range(WINDOW // LANES):
-                lanes = slice(half * LANES, (half + 1) * LANES)
-                for b0 in range(4):
-                    heads = []
-                    for w0 in range(4):
-                        total = None
-                        for w1 in range(4):
-                            w = 4 * w1 + w0
-                            value = quarter(
-                                (grid_ref[w, 0, part, lanes], grid_ref[w, 1, part, lanes]), w1 * b0
-                            )
-                            total = value if total is None else plus(total, value)
-                        total = rotate(total, w0 * b0)
-                        heads.append(total)
-                    even, odd = plus(heads[0], heads[2]), minus(heads[0], heads[2])
-                    even2, odd2 = plus(heads[1], heads[3]), minus(heads[1], heads[3])
-                    odd2 = quarter(odd2, 1)
-                    results = (plus(even, even2), plus(odd, odd2), minus(even, even2), minus(odd, odd2))
-                    for b1, (re, im) in enumerate(results):
-                        b = b0 + 4 * b1
-                        rows = pl.ds(k * LANES + at, 16)
-                        mixed_ref[b, half, rows, :] = re.astype(jnp.bfloat16)
-                        mixed_ref[b, 2 + half, rows, :] = im.astype(jnp.bfloat16)
+        @pl.loop(0, parts)
+        def _(group):
+            fetch(step, k, group).wait()
+            for index in range(2):
+                at = pl.multiple_of(group * 32 + index * 16, 16)
+                part = pl.ds(at, 16)
+                for half in range(WINDOW // LANES):
+                    lanes = slice(half * LANES, (half + 1) * LANES)
+                    for b0 in range(4):
+                        heads = []
+                        for w0 in range(4):
+                            total = None
+                            for w1 in range(4):
+                                w = 4 * w1 + w0
+                                value = quarter(
+                                    (grid_ref[w, 0, part, lanes], grid_ref[w, 1, part, lanes]), w1 * b0
+                                )
+                                total = value if total is None else plus(total, value)
+                            total = rotate(total, w0 * b0)
+                            heads.append(total)
+                        even, odd = plus(heads[0], heads[2]), minus(heads[0], heads[2])
+                        even2, odd2 = plus(heads[1], heads[3]), minus(heads[1], heads[3])
+                        odd2 = quarter(odd2, 1)
+                        results = (plus(even, even2), plus(odd, odd2), minus(even, even2), minus(odd, odd2))
+                        for b1, (re, im) in enumerate(results):
+                            b = b0 + 4 * b1
+                            rows = pl.ds(k * LANES + at, 16)
+                            mixed_ref[b, half, rows, :] = re.astype(jnp.bfloat16)
+                            mixed_ref[b, 2 + half, rows, :] = im.astype(jnp.bfloat16)
+
+    @pl.when((step == 0) & (steps > 1))
+    def _():
+        for k in range(held):
+            for part in range(parts):
+                fetch(step + 1, k, part).start()
 
     def spectrum(b, full_ref):
         mixed = jnp.concatenate([mixed_ref[b, part] for part in range(4)], axis=1)
@@ -587,11 +624,32 @@
                 copy(index, piece).wait()
 
 
-def sum_kernel(own_ref, got_ref, out_ref):
-    for index in range(own_ref.shape[0]):
-        lanes = slice(index * LANES, (index + 1) * LANES)
+def sum_kernel(own_ref, got_ref, image_ref, left_ref, right_ref, out_ref, load_sem, done_sem):
+    steps = left_ref.shape[0]
+
+    def load(index):
+        return (
+            pltpu.make_async_copy(own_ref.at[index], left_ref.at[index], load_sem.at[0, index]),
+            pltpu.make_async_copy(got_ref.at[index], right_ref.at[index], load_sem.at[1, index]),
+        )
+
+    def store(index):
+        lanes = pl.ds(index * LANES, LANES)
+        return pltpu.make_async_copy(
+            out_ref.at[index], image_ref.at[:, :, lanes], done_sem.at[index]
+        )
+
+    for index in range(steps):
+        for copy in load(index):
+            copy.start()
+    for index in range(steps):
+        for copy in load(index):
+            copy.wait()
         for b in range(DIGITS):
-            out_ref[:, b, lanes] = own_ref[index, b] + got_ref[index, b]
+            out_ref[index, :, b, :] = left_ref[index, b] + right_ref[index, b]
+        store(index).start()
+    for index in range(steps):
+        store(index).wait()
 
 
 def local(visibility, target, offset, taps, w_plane):
@@ -620,9 +678,13 @@
             jax.ShapeDtypeStruct((tiles, 3 * blocks + 8, LANES), jnp.float32),
             jax.ShapeDtypeStruct((held, LANES), jnp.float32),
         ],
-        in_specs=[vmem] * 3 + [smem],
+        in_specs=[pl.BlockSpec(memory_space=pl.ANY)] * 3 + [smem],
         out_specs=[vmem] * 2,
         scratch_shapes=[
+            pltpu.VMEM((2, vis_dev), jnp.float32),
+            pltpu.VMEM((vis_dev // LANES, LANES), jnp.int32),
+            pltpu.VMEM((vis_dev // LANES, LANES), jnp.int32),
+            pltpu.SemaphoreType.DMA((3,)),
             pltpu.VMEM((9 * devices, vis_dev), jnp.bfloat16),
             pltpu.VMEM((LANES, vis_dev), jnp.bfloat16),
             pltpu.VMEM((9 * blocks, devices * LANES), jnp.bfloat16),
@@ -655,7 +717,7 @@
         return pl.pallas_call(
             functools.partial(grid_kernel, windows, columns),
             out_shape=jax.ShapeDtypeStruct((DIGITS, 2 * columns, WINDOW), jnp.float32),
-            in_specs=[vmem],
+            in_specs=[pl.BlockSpec(memory_space=pl.ANY)],
             out_specs=pl.BlockSpec(memory_space=pl.ANY),
             scratch_shapes=[
                 pltpu.VMEM((WIDE // LANES, 2 * columns + 16, LANES), jnp.bfloat16),
@@ -663,7 +725,9 @@
                 pltpu.VMEM((2, BLOCK + 8, WIDE + LANES), jnp.float32),
                 pltpu.VMEM((2, 8, WIDE), jnp.float32),
                 pltpu.VMEM((2, 2 * columns, WINDOW), jnp.float32),
+                pltpu.VMEM((tiles, 3 * blocks + 8, LANES), jnp.float32),
                 pltpu.SemaphoreType.DMA((2,)),
+                pltpu.SemaphoreType.DMA((tiles,)),
             ],
             cost_estimate=pl.CostEstimate(
                 flops=2 * slots * tiles * columns * WINDOW, bytes_accessed=1 << 24, transcendentals=0
@@ -697,7 +761,7 @@
             pltpu.VMEM((2, held, DIGITS, 2, LANES, WINDOW), jnp.float32),
             pltpu.SemaphoreType.DMA((steps, DIGITS // PIECE)),
             pltpu.SemaphoreType.DMA((steps, DIGITS // PIECE)),
-            pltpu.SemaphoreType.DMA((2, held)),
+            pltpu.SemaphoreType.DMA((2, held, LANES // 32)),
         ],
         compiler_params=pltpu.CompilerParams(
             collective_id=0,
@@ -706,13 +770,19 @@
             dimension_semantics=("arbitrary",),
         ),
     )(taps, level, *grids)
-    block = pl.BlockSpec((steps // 2, DIGITS, own, LANES), lambda j: (j, 0, 0, 0))
+    anywhere = pl.BlockSpec(memory_space=pl.ANY)
     image = pl.pallas_call(
         sum_kernel,
-        grid=(2,),
         out_shape=jax.ShapeDtypeStruct((own, DIGITS, columns), jnp.float32),
-        in_specs=[block, block],
-        out_specs=pl.BlockSpec((own, DIGITS, columns // 2), lambda j: (0, 0, j)),
+        in_specs=[anywhere] * 2,
+        out_specs=anywhere,
+        scratch_shapes=[
+            pltpu.VMEM((steps, DIGITS, own, LANES), jnp.float32),
+            pltpu.VMEM((steps, DIGITS, own, LANES), jnp.float32),
+            pltpu.VMEM((steps, own, DIGITS, LANES), jnp.float32),
+            pltpu.SemaphoreType.DMA((2, steps)),
+            pltpu.SemaphoreType.DMA((steps,)),
+        ],
     )(mine_part, other_part)
     return image.reshape(own * DIGITS, columns)
 

time: 109 us -> 108 us (level)
    pallas_call x1, Pallas kernels: 4.67 us -> 3.45 us  [local(): pl.pallas_call(sum_kernel, out_shape=jax.ShapeDtypeStruct((own, DIGITS, c...]
  transfers between devices with their start and end apart: 1 -> 1, of which waited for: 0 -> 0; matrix products, arithmetic and copies ran while one was open for 0% -> 0% of each run, Pallas kernels for 21% -> 20%
where the time goes in v2:
time: 108 us; the launch traced here: 106 us
  Pallas kernels  104 us (96%)
  starting transfers between devices  1.33 us (1%)
    pallas_call x2, Pallas kernels, transform(): pl.pallas_call(functools.partial(grid_kernel, windows, columns), out_shap...  43.9 us
    pallas_call x1, Pallas kernels, local(): pl.pallas_call(functools.partial(image_kernel, held, own, columns, 1.0 /...  34.6 us
    pallas_call x1, Pallas kernels, local(): pl.pallas_call(functools.partial(front_kernel, windows, tiles, jumps), ou...  21.6 us
    pallas_call x1, Pallas kernels, local(): pl.pallas_call(sum_kernel, out_shape=jax.ShapeDtypeStruct((own, DIGITS, c...  3.45 us
  transfers between devices with their start and end apart: 1, of which 0 were waited for; matrix products, arithmetic and copies ran while one was open for 0% of the time, Pallas kernels for 20%

profile of v2, /device:TPU:0, one launch (start us, length us, event | category | flops | bytes accessed | tf_op | source)
XLA Modules:
  0.0 106.4 jit_solution(14558048818129712132)
XLA Ops:
  0.7 21.6 %shard_map.55 = (f32[8,104,128]{2,1,0:T(8,128)}, f32[2,128]{1,0:T(2,128)}) custom-call(f32[2,2048]{1,0:T(2,128)} %vis_in.1, s32[16,128]{1,0:T(8,128)} %bitcast.7, s32[16,128]{1,0:T(8,128)} %bitcast.8, f32[1]{0:T(128)S(6)} %copy.6.w_ref), custom_call_target="tpu_custom_call" | custom-call | tf_op jit(solution)/shard_map/pallas_call | solution.py:675
  22.3 1.3 %collective-permute-start = (f32[8,104,128]{2,1,0:T(8,128)}, f32[8,104,128]{2,1,0:T(8,128)S(1)}, u32[]{:S(2)}, u32[]{:S(2)}) collective-permute-start(f32[8,104,128]{2,1,0:T(8,128)} %get-tuple-element.10.list_ref), channel_id=1, source_target_pairs={{0,16},{1,9},{2,18},{3,11},{4,20},{5,13},{6,22},{7,15},{8,24},{9,1... | collective-permute-start | bytes 1277960 | tf_op jit(solution)/shard_map/ppermute | solution.py:714
  23.6 21.7 %shard_map.56 = f32[16,1024,256]{2,1,0:T(8,128)} custom-call(f32[8,104,128]{2,1,0:T(8,128)} %get-tuple-element.10.list_ref), custom_call_target="tpu_custom_call" | custom-call | flops 8589934592 | bytes 16777216 | tf_op jit(solution)/shard_map/pallas_call | solution.py:717
  45.3 0.0 collective-permute-done.list_ref
  45.3 0.0 copy-start
  45.3 0.7 copy-done
  46.0 22.2 %shard_map.57 = f32[16,1024,256]{2,1,0:T(8,128)} custom-call(f32[8,104,128]{2,1,0:T(8,128)} %copy-done), custom_call_target="tpu_custom_call" | custom-call | flops 8589934592 | bytes 16777216 | tf_op jit(solution)/shard_map/pallas_call | solution.py:717
  68.2 34.6 %shard_map.58 = (f32[4,16,64,128]{3,2,1,0:T(8,128)}, f32[4,16,64,128]{3,2,1,0:T(8,128)}) custom-call(f32[8]{0:T(128)} %taps_ref.1, f32[2,128]{1,0:T(2,128)} %get-tuple-element.9.w_ref, f32[16,2,512,256]{3,2,1,0:T(8,128)} %bitcast.5, f32[16,2,512,256]{3,2,1,0:T(8,128)} %bitcast.6), custom_call_target="tpu_custom_call" | custom-call | tf_op jit(solution)/shard_map/pallas_call | solution.py:740
  102.8 3.5 %shard_map.59 = f32[64,16,512]{2,1,0:T(8,128)} custom-call(f32[4,16,64,128]{3,2,1,0:T(8,128)} %get-tuple-element.11.own_ref, f32[4,16,64,128]{3,2,1,0:T(8,128)} %get-tuple-element.12.got_ref), custom_call_target="tpu_custom_call" | custom-call | tf_op jit(solution)/shard_map/pallas_call | solution.py:774
Async XLA Ops:
  22.3 23.0 %collective-permute-start = (f32[8,104,128]{2,1,0:T(8,128)}, f32[8,104,128]{2,1,0:T(8,128)S(1)}, u32[]{:S(2)}, u32[]{:S(2)}) collective-permute-start(f32[8,104,128]{2,1,0:T(8,128)} %get-tuple-element.10.list_ref), channel_id=1, source_target_pairs={{0,16},{1,9},{2,18},{3,11},{4,20},{5,13},{6,22},{7,15},{8,24},{9,1... | collective-permute-start | bytes 1277960 | tf_op jit(solution)/shard_map/ppermute | solution.py:714
  45.3 0.8 copy-start

commit v3 on v2

--- a/solution.py
+++ b/solution.py
@@ -18,6 +18,7 @@
 WIDE = 1024
 HALF = 512
 NARROW = 256
+LARGE = WIDE + NARROW
 MESH = pl.DeviceIdType.MESH
 
 
@@ -387,28 +388,28 @@
     def _():
         chunk(place(0, HALF + NARROW), HALF + NARROW, False)
 
-    @pl.when(number > HALF + NARROW)
-    def _():
-        chunk(place(0, WIDE), WIDE, False)
-
     rest = jnp.maximum(number - WIDE, 0)
     full = rest // WIDE
     tail = rest - full * WIDE
+    short = (tail > 0) & (tail <= NARROW)
     full = full + jnp.where(tail > HALF, 1, 0)
+    begin = jnp.where(short, LARGE // LANES, WIDE // LANES)
+
+    @pl.when((number > HALF + NARROW) & jnp.logical_not(short))
+    def _():
+        chunk(place(0, WIDE), WIDE, False)
+
+    @pl.when(short)
+    def _():
+        chunk(place(0, LARGE), LARGE, False)
 
     @pl.loop(0, full)
     def _(index):
-        chunk(place((index + 1) * (WIDE // LANES), WIDE), WIDE, True)
-
-    done = (full + 1) * (WIDE // LANES)
+        chunk(place(begin + index * (WIDE // LANES), WIDE), WIDE, True)
 
     @pl.when((tail > NARROW) & (tail <= HALF))
     def _():
-        chunk(place(done, HALF), HALF, True)
-
-    @pl.when((tail > 0) & (tail <= NARROW))
-    def _():
-        chunk(place(done, NARROW), NARROW, True)
+        chunk(place(begin + full * (WIDE // LANES), HALF), HALF, True)
 
 
 def place(lane, first, second, count):
@@ -720,10 +721,10 @@
             in_specs=[pl.BlockSpec(memory_space=pl.ANY)],
             out_specs=pl.BlockSpec(memory_space=pl.ANY),
             scratch_shapes=[
-                pltpu.VMEM((WIDE // LANES, 2 * columns + 16, LANES), jnp.bfloat16),
-                pltpu.VMEM((WIDE // LANES, WINDOW + 16, LANES), jnp.bfloat16),
-                pltpu.VMEM((2, BLOCK + 8, WIDE + LANES), jnp.float32),
-                pltpu.VMEM((2, 8, WIDE), jnp.float32),
+                pltpu.VMEM((LARGE // LANES, 2 * columns + 16, LANES), jnp.bfloat16),
+                pltpu.VMEM((LARGE // LANES, WINDOW + 16, LANES), jnp.bfloat16),
+                pltpu.VMEM((2, BLOCK + 8, LARGE + LANES), jnp.float32),
+                pltpu.VMEM((2, 8, LARGE), jnp.float32),
                 pltpu.VMEM((2, 2 * columns, WINDOW), jnp.float32),
                 pltpu.VMEM((tiles, 3 * blocks + 8, LANES), jnp.float32),
                 pltpu.SemaphoreType.DMA((2,)),

time: 108 us -> 107 us (level)
    pallas_call x2, Pallas kernels: 43.9 us -> 42 us  [transform(): pl.pallas_call(functools.partial(grid_kernel, windows, columns), out_shap...]
  transfers between devices with their start and end apart: 1 -> 1, of which waited for: 0 -> 0; matrix products, arithmetic and copies ran while one was open for 0% -> 0% of each run, Pallas kernels for 20% -> 19%
where the time goes in v3:
time: 107 us; the launch traced here: 106 us
  Pallas kernels  103 us (96%)
  starting transfers between devices  1.33 us (1%)
    pallas_call x2, Pallas kernels, transform(): pl.pallas_call(functools.partial(grid_kernel, windows, columns), out_shap...  42 us
    pallas_call x1, Pallas kernels, local(): pl.pallas_call(functools.partial(image_kernel, held, own, columns, 1.0 /...  35.5 us
    pallas_call x1, Pallas kernels, local(): pl.pallas_call(functools.partial(front_kernel, windows, tiles, jumps), ou...  21.6 us
    pallas_call x1, Pallas kernels, local(): pl.pallas_call(sum_kernel, out_shape=jax.ShapeDtypeStruct((own, DIGITS, c...  3.45 us
  transfers between devices with their start and end apart: 1, of which 0 were waited for; matrix products, arithmetic and copies ran while one was open for 0% of the time, Pallas kernels for 19%

profile of v3, /device:TPU:0, one launch (start us, length us, event | category | flops | bytes accessed | tf_op | source)
XLA Modules:
  0.0 105.5 jit_solution(8828950404482761576)
XLA Ops:
  0.7 21.6 %shard_map.55 = (f32[8,104,128]{2,1,0:T(8,128)}, f32[2,128]{1,0:T(2,128)}) custom-call(f32[2,2048]{1,0:T(2,128)} %vis_in.1, s32[16,128]{1,0:T(8,128)} %bitcast.7, s32[16,128]{1,0:T(8,128)} %bitcast.8, f32[1]{0:T(128)S(6)} %copy.6.w_ref), custom_call_target="tpu_custom_call" | custom-call | tf_op jit(solution)/shard_map/pallas_call | solution.py:676
  22.3 1.3 %collective-permute-start = (f32[8,104,128]{2,1,0:T(8,128)}, f32[8,104,128]{2,1,0:T(8,128)S(1)}, u32[]{:S(2)}, u32[]{:S(2)}) collective-permute-start(f32[8,104,128]{2,1,0:T(8,128)} %get-tuple-element.10.list_ref), channel_id=1, source_target_pairs={{0,16},{1,9},{2,18},{3,11},{4,20},{5,13},{6,22},{7,15},{8,24},{9,1... | collective-permute-start | bytes 1277960 | tf_op jit(solution)/shard_map/ppermute | solution.py:715
  23.6 20.3 %shard_map.56 = f32[16,1024,256]{2,1,0:T(8,128)} custom-call(f32[8,104,128]{2,1,0:T(8,128)} %get-tuple-element.10.list_ref), custom_call_target="tpu_custom_call" | custom-call | flops 8589934592 | bytes 16777216 | tf_op jit(solution)/shard_map/pallas_call | solution.py:718
  43.9 0.0 collective-permute-done.list_ref
  43.9 0.0 copy-start
  43.9 0.7 copy-done
  44.7 21.7 %shard_map.57 = f32[16,1024,256]{2,1,0:T(8,128)} custom-call(f32[8,104,128]{2,1,0:T(8,128)} %copy-done), custom_call_target="tpu_custom_call" | custom-call | flops 8589934592 | bytes 16777216 | tf_op jit(solution)/shard_map/pallas_call | solution.py:718
  66.3 35.5 %shard_map.58 = (f32[4,16,64,128]{3,2,1,0:T(8,128)}, f32[4,16,64,128]{3,2,1,0:T(8,128)}) custom-call(f32[8]{0:T(128)} %taps_ref.1, f32[2,128]{1,0:T(2,128)} %get-tuple-element.9.w_ref, f32[16,2,512,256]{3,2,1,0:T(8,128)} %bitcast.5, f32[16,2,512,256]{3,2,1,0:T(8,128)} %bitcast.6), custom_call_target="tpu_custom_call" | custom-call | tf_op jit(solution)/shard_map/pallas_call | solution.py:741
  101.9 3.5 %shard_map.59 = f32[64,16,512]{2,1,0:T(8,128)} custom-call(f32[4,16,64,128]{3,2,1,0:T(8,128)} %get-tuple-element.11.own_ref, f32[4,16,64,128]{3,2,1,0:T(8,128)} %get-tuple-element.12.got_ref), custom_call_target="tpu_custom_call" | custom-call | tf_op jit(solution)/shard_map/pallas_call | solution.py:775
Async XLA Ops:
  22.3 21.6 %collective-permute-start = (f32[8,104,128]{2,1,0:T(8,128)}, f32[8,104,128]{2,1,0:T(8,128)S(1)}, u32[]{:S(2)}, u32[]{:S(2)}) collective-permute-start(f32[8,104,128]{2,1,0:T(8,128)} %get-tuple-element.10.list_ref), channel_id=1, source_target_pairs={{0,16},{1,9},{2,18},{3,11},{4,20},{5,13},{6,22},{7,15},{8,24},{9,1... | collective-permute-start | bytes 1277960 | tf_op jit(solution)/shard_map/ppermute | solution.py:715
  43.9 0.8 copy-start
